TPU v7x, 32 devices: a 4x2x2 block of a 4x4x8 slice. The times are simulated.
32 devices in a mesh: dp: 4 (over y, z), sp: 8 (over x, core).
Axes of the slice: x: 4, y: 2, z: 2, core: 2. Of those that a mesh axis runs over, the one named last changes fastest.
The devices are a block of a 4x4x8 slice.
Arguments:
- tokens: bfloat16 [24, 4096, 2560], P('dp', 'sp'), parts along dimension 0
- w_query: bfloat16 [2560, 4096], replicated
- w_key: bfloat16 [2560, 1024], replicated
- w_value: bfloat16 [2560, 1024], replicated
- w_out: bfloat16 [4096, 2560], replicated
- attn_norm: bfloat16 [2560], replicated
- q_norm: bfloat16 [128], replicated
- k_norm: bfloat16 [128], replicated
Outputs:
- output 1: bfloat16 [24, 4096, 2560], P('dp', 'sp'), parts along dimension 0
- output 2: bfloat16 [24, 4096, 8, 128], P('dp', 'sp'), parts along dimension 0
- output 3: bfloat16 [24, 4096, 8, 128], P('dp', 'sp'), parts along dimension 0
There are 4 independent parts. A program takes and returns all parts, laid end to end along the dimension named above; an argument that names none is the same for every part.
All inputs are finite; a program needn't handle non-finite values.
Results may differ from a plain program's by a relative error of at most 0.00828171.
Values are sent between devices in bfloat16 or wider.
A program may use at most 768 MiB of HBM per device.

v0:
```python
import jax
import jax.numpy as jnp
from jax import lax
from jax.sharding import PartitionSpec as P

EPS = 1e-6
THETA = 1000000.0
HEAD_DIM = 128


def rms_norm(values, gain_vec):
    wide_vals = values.astype(jnp.float32)
    inv_rms = lax.rsqrt(jnp.mean(wide_vals * wide_vals, axis=-1, keepdims=True) + EPS)
    return wide_vals * inv_rms * gain_vec.astype(jnp.float32)


def rope_rotate(values, positions):
    half_dim = HEAD_DIM // 2
    inv_freq = THETA ** (-jnp.arange(half_dim, dtype=jnp.float32) * 2.0 / HEAD_DIM)
    angles = positions.astype(jnp.float32)[:, None] * inv_freq[None, :]
    cos_t = jnp.cos(angles)[None, :, None, :]
    sin_t = jnp.sin(angles)[None, :, None, :]
    lo_half = values[..., :half_dim]
    hi_half = values[..., half_dim:]
    return jnp.concatenate([lo_half * cos_t - hi_half * sin_t, hi_half * cos_t + lo_half * sin_t], axis=-1)


def qkv_local(tokens, w_query, w_key, w_value, attn_norm, q_norm, k_norm, positions):
    n_batch, n_tok, d_model = tokens.shape
    hidden = rms_norm(tokens, attn_norm).astype(jnp.bfloat16).reshape(n_batch * n_tok, d_model)

    def project(weight):
        flat_out = jnp.dot(hidden, weight, preferred_element_type=jnp.float32).astype(jnp.bfloat16)
        return flat_out.reshape(n_batch, n_tok, weight.shape[1] // HEAD_DIM, HEAD_DIM)

    q_rot = rope_rotate(rms_norm(project(w_query), q_norm), positions).astype(jnp.bfloat16)
    k_rot = rope_rotate(rms_norm(project(w_key), k_norm), positions).astype(jnp.bfloat16)
    return q_rot, k_rot, project(w_value)


def finish_block(tokens, attn_heads, w_out):
    n_batch, n_tok, d_model = tokens.shape
    flat_in = attn_heads.reshape(n_batch * n_tok, w_out.shape[0])
    proj_out = jnp.dot(flat_in, w_out, preferred_element_type=jnp.float32).reshape(n_batch, n_tok, d_model)
    return (tokens.astype(jnp.float32) + proj_out).astype(jnp.bfloat16)


def causal_attention(q_group, k_seq, v_seq, q_offset):
    n_batch, q_len, n_kv, n_group, head_dim = q_group.shape
    blk_len = min(256, q_len)
    n_qblk = q_len // blk_len
    scale = head_dim ** -0.5
    q_blocks = q_group.reshape(n_batch, n_qblk, blk_len, n_kv, n_group, head_dim)
    row_ids = jnp.arange(blk_len)
    stat_shape = (n_batch, blk_len, n_kv, n_group)

    def one_block(blk_idx):
        q_blk = lax.dynamic_index_in_dim(q_blocks, blk_idx, axis=1, keepdims=False)
        q_start = q_offset + blk_idx * blk_len
        n_kblk = q_start // blk_len + 1

        def key_step(key_blk, carry):
            run_max, run_sum, out_acc = carry
            k_blk = lax.dynamic_slice_in_dim(k_seq, key_blk * blk_len, blk_len, axis=1)
            v_blk = lax.dynamic_slice_in_dim(v_seq, key_blk * blk_len, blk_len, axis=1)
            scores = jnp.einsum('bqkgd,bskd->bqkgs', q_blk, k_blk, preferred_element_type=jnp.float32) * scale
            allowed = (key_blk * blk_len + row_ids)[None, :] <= (q_start + row_ids)[:, None]
            scores = jnp.where(allowed[None, :, None, None, :], scores, -jnp.inf)
            new_max = jnp.maximum(run_max, jnp.max(scores, axis=-1))
            rescale = jnp.exp(run_max - new_max)
            probs_blk = jnp.exp(scores - new_max[..., None])
            run_sum = run_sum * rescale + jnp.sum(probs_blk, axis=-1)
            out_acc = out_acc * rescale[..., None] + jnp.einsum('bqkgs,bskd->bqkgd', probs_blk.astype(jnp.bfloat16), v_blk, preferred_element_type=jnp.float32)
            return new_max, run_sum, out_acc

        init_state = (jnp.full(stat_shape, -jnp.inf, jnp.float32), jnp.zeros(stat_shape, jnp.float32), jnp.zeros(stat_shape + (head_dim,), jnp.float32))
        final_state = lax.fori_loop(0, n_kblk, key_step, init_state)
        return (final_state[2] / final_state[1][..., None]).astype(jnp.bfloat16)

    attn_blocks = lax.map(one_block, jnp.arange(n_qblk))
    return jnp.moveaxis(attn_blocks, 0, 1).reshape(n_batch, q_len, n_kv, n_group, head_dim)


def solution(mesh):
    n_sp = mesh.shape['sp']

    def per_device(tokens, w_query, w_key, w_value, w_out, attn_norm, q_norm, k_norm):
        n_batch, seq_loc, d_model = tokens.shape
        positions = lax.axis_index('sp') * seq_loc + jnp.arange(seq_loc)
        q_rot, k_rot, v_proj = qkv_local(tokens, w_query, w_key, w_value, attn_norm, q_norm, k_norm, positions)
        n_kv = k_rot.shape[2]
        copies = max(1, n_sp // n_kv)
        k_send = jnp.repeat(k_rot, copies, axis=2) if copies > 1 else k_rot
        v_send = jnp.repeat(v_proj, copies, axis=2) if copies > 1 else v_proj
        q_heads = lax.all_to_all(q_rot, 'sp', 2, 1, tiled=True)
        k_heads = lax.all_to_all(k_send, 'sp', 2, 1, tiled=True)
        v_heads = lax.all_to_all(v_send, 'sp', 2, 1, tiled=True)
        seq_len = q_heads.shape[1]
        h_loc = q_heads.shape[2]
        kv_loc = k_heads.shape[2]
        attn_out = causal_attention(q_heads.reshape(n_batch, seq_len, kv_loc, h_loc // kv_loc, HEAD_DIM), k_heads, v_heads, 0)
        attn_seq = lax.all_to_all(attn_out.reshape(n_batch, seq_len, h_loc, HEAD_DIM), 'sp', 1, 2, tiled=True)
        return finish_block(tokens, attn_seq, w_out), k_rot, v_proj

    spec_tok = P('dp', 'sp', None)
    spec_cache = P('dp', 'sp', None, None)
    spec_mat = P(None, None)
    spec_vec = P(None)
    return jax.shard_map(per_device, mesh=mesh, in_specs=(spec_tok, spec_mat, spec_mat, spec_mat, spec_mat, spec_vec, spec_vec, spec_vec), out_specs=(spec_tok, spec_cache, spec_cache), check_vma=False)
```

profile of v0, /device:TPU:81, one launch (start us, length us, event | category | flops | bytes accessed | tf_op | source)
XLA Modules:
  0.0 2334.1 jit_solution(13345493676168002412)
XLA Ops:
  0.7 8.5 fusion.27
  15.0 5.8 copy-done.2
  20.8 18.8 convert_bitcast_fusion.1
  39.6 12.3 copy.74
  51.8 8.0 multiply_reduce_fusion.1
  61.4 9.5 fusion.33
  70.9 4.4 subtract_convert_fusion.1
  75.4 4.9 pad_maximum_fusion.1
  80.3 6.7 all-to-all-start.1
  87.0 74.7 %convert_bitcast_fusion = f32[384,8,32,128]{3,1,2,0:T(8,128)} fusion(bf16[3072,2560]{1,0:T(8,128)(2,1)} %bitcast.153, bf16[2560,4096]{1,0:T(8,128)(2,1)} %param.13), kind=kOutput, calls=%fused_computation.36 | convolution fusion | flops 64449675264 | bytes 87031808 | tf_op jit(solution)/shard_map/dot_general | solution.py:33
  161.6 41.0 %copy.73 = f32[384,8,32,128]{3,2,1,0:T(8,128)} copy(f32[384,8,32,128]{3,1,2,0:T(8,128)} %convert_bitcast_fusion) | data formatting | bytes 100663296
  202.6 16.9 multiply_reduce_fusion
  220.3 20.8 convert_bitcast_fusion.2
  249.8 4.9 all-to-all-start.2
  254.7 33.9 %fusion.26 = f32[6,512,32,128]{3,1,0,2:T(8,128)} fusion(f32[6,512,32,128]{3,2,1,0:T(8,128)} %bitcast.139, f32[128]{0:T(128)S(1)} %convert_element_type.65, f32[6,512,32]{1,0,2:T(8,128)S(1)} %copy.49), kind=kLoop, calls=%fused_computation.35 | loop fusion | flops 25165824 | bytes 101057024 | tf_op jit(solution)/shard_map/mul | solution.py:14
  288.6 49.7 %subtract_convert_fusion = (bf16[6,512,32,64]{3,1,0,2:T(8,128)(2,1)}, bf16[6,512,32,64]{3,1,0,2:T(8,128)(2,1)}) fusion(f32[6,512,32,128]{3,1,0,2:T(8,128)} %fusion.26, f32[512,64]{1,0:T(8,128)S(1)} %copy-done.6, f32[512,64]{1,0:T(8,128)S(1)} %copy-done.4), kind=kLoop, calls=%fused_computation.38 | loop fusion | flops 50331648 | bytes 75759616 | tf_op jit(solution)/shard_map/convert.4
  338.3 30.6 %pad_maximum_fusion = bf16[6,512,32,128]{3,1,0,2:T(8,128)(2,1)} fusion(bf16[6,512,32,64]{3,1,0,2:T(8,128)(2,1)} %get-tuple-element.290, bf16[6,512,32,64]{3,1,0,2:T(8,128)(2,1)} %get-tuple-element.289), kind=kLoop, calls=%fused_computation.47 | loop fusion | flops 50331648 | bytes 50331648 | tf_op jit(solution)/shard_map/concatenate | solution.py:25
  368.9 7.3 all-to-all-start
  376.2 6.2 copy.58
  382.4 8.6 copy.60
  391.0 6.2 copy.56
  397.2 252.2 %all-to-all-done = bf16[6,512,32,128]{3,1,0,2:T(8,128)(2,1)} async-done(((bf16[6,512,32,128]{3,1,0,2:T(8,128)(2,1)}), bf16[6,512,32,128]{3,1,0,2:T(8,128)(2,1)}, u32[]{:S(2)}, u32[]{:S(2)}) %all-to-all-start) | async-done | bytes 25165856 | tf_op jit(solution)/shard_map/all_to_all | solution.py:95
  649.4 20.8 copy.52
  670.2 1179.9 %while.44 = (s32[]{:T(128)}, bf16[16,6,256,1,4,128]{5,2,0,4,1,3:T(8,128)(2,1)}, s32[16]{0:T(128)S(1)}, bf16[6,16,256,1,4,128]{5,2,1,4,0,3:T(8,128)(2,1)}, bf16[6...) while((s32[]{:T(128)}, ...), condition=%wide.region_8.9_spmd.clone.clone, body=%wide.region_3.8_spmd.clone.clone.sunk | while | flops 825838080 | bytes 45563092 | solution.py:80
  676.7 7.3 while.45
  695.4 14.7 while.45
  721.5 22.0 while.45
  754.9 29.4 %while.45 = (s32[]{:T(128)}, f32[6,256,1,4]{1,3,0,2:T(4,128)S(1)}, f32[6,256,1,4]{1,3,0,2:T(4,128)S(1)}, f32[6,256,1,4,128]{1,4,3,0,2:T(8,128)S(1)}, s32[]{:T(12...) while((s32[]{:T(128)}, f32[6,256,1,4]{1,3,0,2:T(4,128)S(1)}, ...), condition=%wide.region_7.7_spmd.clone, body=%wide.region_4.6_spmd.clone.sunk | while | flops 824265216 | bytes 28185796 | solution.py:77
  795.6 36.7 %while.45 = (s32[]{:T(128)}, f32[6,256,1,4]{1,3,0,2:T(4,128)S(1)}, f32[6,256,1,4]{1,3,0,2:T(4,128)S(1)}, f32[6,256,1,4,128]{1,4,3,0,2:T(8,128)S(1)}, s32[]{:T(12...) while((s32[]{:T(128)}, f32[6,256,1,4]{1,3,0,2:T(4,128)S(1)}, ...), condition=%wide.region_7.7_spmd.clone, body=%wide.region_4.6_spmd.clone.sunk | while | flops 824265216 | bytes 28185796 | solution.py:77
  843.6 44.0 %while.45 = (s32[]{:T(128)}, f32[6,256,1,4]{1,3,0,2:T(4,128)S(1)}, f32[6,256,1,4]{1,3,0,2:T(4,128)S(1)}, f32[6,256,1,4,128]{1,4,3,0,2:T(8,128)S(1)}, s32[]{:T(12...) while((s32[]{:T(128)}, f32[6,256,1,4]{1,3,0,2:T(4,128)S(1)}, ...), condition=%wide.region_7.7_spmd.clone, body=%wide.region_4.6_spmd.clone.sunk | while | flops 824265216 | bytes 28185796 | solution.py:77
  899.0 51.4 %while.45 = (s32[]{:T(128)}, f32[6,256,1,4]{1,3,0,2:T(4,128)S(1)}, f32[6,256,1,4]{1,3,0,2:T(4,128)S(1)}, f32[6,256,1,4,128]{1,4,3,0,2:T(8,128)S(1)}, s32[]{:T(12...) while((s32[]{:T(128)}, f32[6,256,1,4]{1,3,0,2:T(4,128)S(1)}, ...), condition=%wide.region_7.7_spmd.clone, body=%wide.region_4.6_spmd.clone.sunk | while | flops 824265216 | bytes 28185796 | solution.py:77
  961.7 58.7 %while.45 = (s32[]{:T(128)}, f32[6,256,1,4]{1,3,0,2:T(4,128)S(1)}, f32[6,256,1,4]{1,3,0,2:T(4,128)S(1)}, f32[6,256,1,4,128]{1,4,3,0,2:T(8,128)S(1)}, s32[]{:T(12...) while((s32[]{:T(128)}, f32[6,256,1,4]{1,3,0,2:T(4,128)S(1)}, ...), condition=%wide.region_7.7_spmd.clone, body=%wide.region_4.6_spmd.clone.sunk | while | flops 824265216 | bytes 28185796 | solution.py:77
  1031.8 66.1 %while.45 = (s32[]{:T(128)}, f32[6,256,1,4]{1,3,0,2:T(4,128)S(1)}, f32[6,256,1,4]{1,3,0,2:T(4,128)S(1)}, f32[6,256,1,4,128]{1,4,3,0,2:T(8,128)S(1)}, s32[]{:T(12...) while((s32[]{:T(128)}, f32[6,256,1,4]{1,3,0,2:T(4,128)S(1)}, ...), condition=%wide.region_7.7_spmd.clone, body=%wide.region_4.6_spmd.clone.sunk | while | flops 824265216 | bytes 28185796 | solution.py:77
  1109.2 73.4 %while.45 = (s32[]{:T(128)}, f32[6,256,1,4]{1,3,0,2:T(4,128)S(1)}, f32[6,256,1,4]{1,3,0,2:T(4,128)S(1)}, f32[6,256,1,4,128]{1,4,3,0,2:T(8,128)S(1)}, s32[]{:T(12...) while((s32[]{:T(128)}, f32[6,256,1,4]{1,3,0,2:T(4,128)S(1)}, ...), condition=%wide.region_7.7_spmd.clone, body=%wide.region_4.6_spmd.clone.sunk | while | flops 824265216 | bytes 28185796 | solution.py:77
  1193.9 80.7 %while.45 = (s32[]{:T(128)}, f32[6,256,1,4]{1,3,0,2:T(4,128)S(1)}, f32[6,256,1,4]{1,3,0,2:T(4,128)S(1)}, f32[6,256,1,4,128]{1,4,3,0,2:T(8,128)S(1)}, s32[]{:T(12...) while((s32[]{:T(128)}, f32[6,256,1,4]{1,3,0,2:T(4,128)S(1)}, ...), condition=%wide.region_7.7_spmd.clone, body=%wide.region_4.6_spmd.clone.sunk | while | flops 824265216 | bytes 28185796 | solution.py:77
  1286.0 88.1 %while.45 = (s32[]{:T(128)}, f32[6,256,1,4]{1,3,0,2:T(4,128)S(1)}, f32[6,256,1,4]{1,3,0,2:T(4,128)S(1)}, f32[6,256,1,4,128]{1,4,3,0,2:T(8,128)S(1)}, s32[]{:T(12...) while((s32[]{:T(128)}, f32[6,256,1,4]{1,3,0,2:T(4,128)S(1)}, ...), condition=%wide.region_7.7_spmd.clone, body=%wide.region_4.6_spmd.clone.sunk | while | flops 824265216 | bytes 28185796 | solution.py:77
  1385.5 95.4 %while.45 = (s32[]{:T(128)}, f32[6,256,1,4]{1,3,0,2:T(4,128)S(1)}, f32[6,256,1,4]{1,3,0,2:T(4,128)S(1)}, f32[6,256,1,4,128]{1,4,3,0,2:T(8,128)S(1)}, s32[]{:T(12...) while((s32[]{:T(128)}, f32[6,256,1,4]{1,3,0,2:T(4,128)S(1)}, ...), condition=%wide.region_7.7_spmd.clone, body=%wide.region_4.6_spmd.clone.sunk | while | flops 824265216 | bytes 28185796 | solution.py:77
  1492.3 102.7 %while.45 = (s32[]{:T(128)}, f32[6,256,1,4]{1,3,0,2:T(4,128)S(1)}, f32[6,256,1,4]{1,3,0,2:T(4,128)S(1)}, f32[6,256,1,4,128]{1,4,3,0,2:T(8,128)S(1)}, s32[]{:T(12...) while((s32[]{:T(128)}, f32[6,256,1,4]{1,3,0,2:T(4,128)S(1)}, ...), condition=%wide.region_7.7_spmd.clone, body=%wide.region_4.6_spmd.clone.sunk | while | flops 824265216 | bytes 28185796 | solution.py:77
  1606.4 110.1 %while.45 = (s32[]{:T(128)}, f32[6,256,1,4]{1,3,0,2:T(4,128)S(1)}, f32[6,256,1,4]{1,3,0,2:T(4,128)S(1)}, f32[6,256,1,4,128]{1,4,3,0,2:T(8,128)S(1)}, s32[]{:T(12...) while((s32[]{:T(128)}, f32[6,256,1,4]{1,3,0,2:T(4,128)S(1)}, ...), condition=%wide.region_7.7_spmd.clone, body=%wide.region_4.6_spmd.clone.sunk | while | flops 824265216 | bytes 28185796 | solution.py:77
  1727.8 117.4 %while.45 = (s32[]{:T(128)}, f32[6,256,1,4]{1,3,0,2:T(4,128)S(1)}, f32[6,256,1,4]{1,3,0,2:T(4,128)S(1)}, f32[6,256,1,4,128]{1,4,3,0,2:T(8,128)S(1)}, s32[]{:T(12...) while((s32[]{:T(128)}, f32[6,256,1,4]{1,3,0,2:T(4,128)S(1)}, ...), condition=%wide.region_7.7_spmd.clone, body=%wide.region_4.6_spmd.clone.sunk | while | flops 824265216 | bytes 28185796 | solution.py:77
  1850.1 32.3 %copy.62 = bf16[6,4096,4,128]{3,2,0,1:T(4,128)(2,1)} copy(bf16[6,4096,4,128]{3,1,2,0:T(8,128)(2,1)} %bitcast.148) | data formatting | bytes 50331648 | tf_op jit(solution)/shard_map/reshape;reshape | solution.py:102
  1882.4 7.7 all-to-all-start.3
  1890.1 9.5 copy.65
  1899.7 263.7 %all-to-all-done.3 = bf16[6,4096,4,128]{3,2,0,1:T(4,128)(2,1)} async-done(((bf16[6,4096,4,128]{3,2,0,1:T(4,128)(2,1)}), bf16[6,4096,4,128]{3,2,0,1:T(4,128)(2,1)}, u32[]{:S(2)}, u32[]{:S(2)}) %all-to-all-start.3) | async-done | bytes 25165856 | tf_op jit(solution)/shard_map/all_to_all | solution.py:102
  2163.4 22.4 copy.63
  2185.8 32.2 %copy.64 = bf16[6,512,8,4,128]{4,3,2,1,0:T(4,128)(2,1)} copy(bf16[6,512,8,4,128]{4,1,2,3,0:T(8,128)(2,1)} %bitcast.144) | data formatting | bytes 50331648 | tf_op jit(solution)/shard_map/all_to_all | solution.py:102
  2218.0 41.0 %dot_general.25 = bf16[6,512,4096]{2,1,0:T(8,128)(2,1)} reshape(bf16[6,512,8,4,128]{4,3,2,1,0:T(4,128)(2,1)} %copy.64) | data formatting | bytes 50331648 | tf_op jit(solution)/shard_map/dot_general | solution.py:44
  2259.1 74.8 %fusion.30 = bf16[6,512,2560]{2,1,0:T(8,128)(2,1)} fusion(bf16[6,512,2560]{2,1,0:T(8,128)(2,1)} %param.12, bf16[6,512,4096]{2,1,0:T(8,128)(2,1)} %dot_general.25, bf16[4096,2560]{1,0:T(8,128)(2,1)} %param.16), kind=kOutput, calls=%fused_computation.46 | convolution fusion | flops 64448102400 | bytes 77594624 | tf_op jit(solution)/shard_map/dot_general | solution.py:44
  (1276 shorter events, 1140.4 us)
Async XLA Ops:
  0.6 10.1 copy-start
  0.6 8.6 copy-start.7
  0.7 20.1 slice-start
  10.7 10.0 slice-start.1
  15.0 5.8 copy-start.2
  51.8 8.5 copy-start.8
  61.4 9.5 copy-start.3
  61.4 9.5 copy-start.5
  80.3 169.5 %all-to-all-start.1 = ((bf16[6,512,8,128]{3,1,0,2:T(8,128)(2,1)}), bf16[6,512,8,128]{3,1,0,2:T(8,128)(2,1)}, u32[]{:S(2)}, u32[]{:S(2)}) async-start(bf16[6,512,8,128]{3,1,0,2:T(8,128)(2,1)} %pad_maximum_fusion.1), calls=%async_computation.1 | async-start | bytes 12582912 | tf_op jit(solution)/shard_map/all_to_all | solution.py:96
  202.6 17.7 copy-start.9
  242.8 2.7 copy-start.1
  249.8 119.1 %all-to-all-start.2 = ((bf16[6,512,8,128]{3,1,0,2:T(8,128)(2,1)}), bf16[6,512,8,128]{3,1,0,2:T(8,128)(2,1)}, u32[]{:S(2)}, u32[]{:S(2)}) async-start(bf16[6,512,8,128]{3,1,0,2:T(8,128)(2,1)} %copy.57), calls=%async_computation.2 | async-start | bytes 12582912 | tf_op jit(solution)/shard_map/all_to_all | solution.py:97
  254.7 33.9 %copy-start.4 = (f32[512,64]{1,0:T(8,128)S(1)}, f32[512,64]{1,0:T(8,128)}, u32[]{:S(2)}) copy-start(f32[512,64]{1,0:T(8,128)} %copy-done.3) | copy-start | bytes 393220
  254.7 33.9 %copy-start.6 = (f32[512,64]{1,0:T(8,128)S(1)}, f32[512,64]{1,0:T(8,128)}, u32[]{:S(2)}) copy-start(f32[512,64]{1,0:T(8,128)} %copy-done.5) | copy-start | bytes 393220
  368.9 280.5 %all-to-all-start = ((bf16[6,512,32,128]{3,1,0,2:T(8,128)(2,1)}), bf16[6,512,32,128]{3,1,0,2:T(8,128)(2,1)}, u32[]{:S(2)}, u32[]{:S(2)}) async-start(bf16[6,512,32,128]{3,1,0,2:T(8,128)(2,1)} %pad_maximum_fusion), calls=%async_computation | async-start | bytes 50331648 | tf_op jit(solution)/shard_map/all_to_all | solution.py:95
  1882.4 280.9 %all-to-all-start.3 = ((bf16[6,4096,4,128]{3,2,0,1:T(4,128)(2,1)}), bf16[6,4096,4,128]{3,2,0,1:T(4,128)(2,1)}, u32[]{:S(2)}, u32[]{:S(2)}) async-start(bf16[6,4096,4,128]{3,2,0,1:T(4,128)(2,1)} %copy.62), calls=%async_computation.3 | async-start | bytes 50331648 | tf_op jit(solution)/shard_map/all_to_all | solution.py:102
where the time goes:
time: 2360 us; the launch traced here: 2330 us
  matrix products  976 us (41%)
  waiting for transfers between devices  516 us (22%)
  other arithmetic  396 us (17%)
  local copies, waits for them, and re-layouts  362 us (15%)
  loops' own time  56.1 us (2%)
  starting transfers between devices  26.6 us (1%)
    dot_general x136, matrix products, key_step(): jnp.einsum('bqkgs,bskd->bqkgd', probs_blk.astype(jnp.bfloat16), v_blk, pr...  440 us
    dot_general x136, matrix products, key_step(): jnp.einsum('bqkgd,bskd->bqkgs', q_blk, k_blk, preferred_element_type=jnp....  347 us
    all_to_all x1, waiting for transfers between devices, per_device(): lax.all_to_all(attn_out.reshape(n_batch, seq_len, h_loc, HEAD_DIM), 'sp',...  264 us
    all_to_all x1, waiting for transfers between devices, per_device(): q_heads = lax.all_to_all(q_rot, 'sp', 2, 1, tiled=True)  252 us
    reduce_sum x136, other arithmetic, key_step(): run_sum = run_sum * rescale + jnp.sum(probs_blk, axis=-1)  179 us
    dot_general x3, matrix products, project(): jnp.dot(hidden, weight, preferred_element_type=jnp.float32)  114 us
    unnamed x29, local copies, waits for them, and re-layouts  83.1 us
    dot_general x1, matrix products, finish_block(): jnp.dot(flat_in, w_out, preferred_element_type=jnp.float32)  74.8 us
  transfers between devices with their start and end apart: 4, of which 2 were waited for; matrix products, arithmetic and copies ran while one was open for 13% of the time, Pallas kernels for 0%

commit v1 on v0

v1 whole, which is shorter than its diff:
```python
import functools
import math

import jax
import jax.numpy as jnp
from jax import lax
from jax.experimental import pallas as pl
from jax.experimental.pallas import tpu as pltpu
from jax.sharding import PartitionSpec as P


EPS = 1e-6
THETA = 1000000.0
HEAD_DIM = 128
N_SPLIT = 3
ORDER = [
    ('qkv', 0), ('qkv', 1), ('qkv', 2), ('att', 0), ('qkv', 3), ('att', 1), ('qkv', 4), ('att', 2), ('qkv', 5),
    ('att', 3), ('out', 0), ('out', 1), ('out', 2), ('out', 3), ('att', 4), ('out', 4), ('att', 5), ('out', 5),
]
VMEM_LIMIT = 60 * 1024 * 1024


def rope_tables(positions):
    half_dim = HEAD_DIM // 2
    inv_freq = THETA ** (-jnp.arange(half_dim, dtype=jnp.float32) * 2.0 / HEAD_DIM)
    angles = positions.astype(jnp.float32)[:, None] * inv_freq[None, :]
    cos_t, sin_t = jnp.cos(angles), jnp.sin(angles)
    return jnp.concatenate([cos_t, cos_t], axis=-1), jnp.concatenate([-sin_t, sin_t], axis=-1)


def head_norm_rope(head, gain, cos_t, sin_t):
    wide = head.astype(jnp.float32)
    inv_rms = lax.rsqrt(jnp.mean(wide * wide, axis=-1, keepdims=True) + EPS)
    normed = wide * inv_rms * gain
    return (normed * cos_t + pltpu.roll(normed, HEAD_DIM // 2, 1) * sin_t).astype(jnp.bfloat16)


def qkv_kernel(x_ref, wq_ref, wk_ref, wv_ref, an_ref, qn_ref, kn_ref, cos_ref, sin_ref, *refs):
    send_ref, kc_ref, vc_ref, hid_ref = refs[-4:]
    n_dest, n_slot = send_ref.shape[:2]
    n_group = n_slot - 2
    two = 2 * HEAD_DIM

    @pl.when(pl.program_id(0) == 0)
    def _():
        wide = x_ref[0].astype(jnp.float32)
        inv_rms = lax.rsqrt(jnp.mean(wide * wide, axis=-1, keepdims=True) + EPS)
        hid_ref[...] = (wide * inv_rms * an_ref[...].astype(jnp.float32)).astype(jnp.bfloat16)

    q_gain = qn_ref[...].astype(jnp.float32)
    k_gain = kn_ref[...].astype(jnp.float32)

    def project(weight):
        return jnp.dot(hid_ref[...], weight, preferred_element_type=jnp.float32).astype(jnp.bfloat16)

    def weight_of(job):
        dest, pair = job
        if pair == n_group // 2:
            col = slice(dest * HEAD_DIM, (dest + 1) * HEAD_DIM)
            return jnp.concatenate([wk_ref[:, col], wv_ref[:, col]], axis=1)
        first = dest * n_group * HEAD_DIM + pair * two
        return wq_ref[:, first:first + two]

    def finish(job, both):
        dest, pair = job
        if pair == n_group // 2:
            col = slice(dest * HEAD_DIM, (dest + 1) * HEAD_DIM)
            key = head_norm_rope(both[:, :HEAD_DIM], k_gain, cos_ref[...], sin_ref[...])
            send_ref[dest, n_group] = key
            kc_ref[0, :, col] = key
            send_ref[dest, n_group + 1] = both[:, HEAD_DIM:]
            vc_ref[0, :, col] = both[:, HEAD_DIM:]
            return
        for sub in range(2):
            head = both[:, sub * HEAD_DIM:(sub + 1) * HEAD_DIM]
            send_ref[dest, 2 * pair + sub] = head_norm_rope(head, q_gain, cos_ref[...], sin_ref[...])

    jobs = [(dest, pair) for dest in range(n_dest) for pair in range(n_group // 2 + 1)]
    pending = None
    for job in jobs:
        both = project(weight_of(job))
        if pending is not None:
            finish(*pending)
        pending = (job, both)
    finish(*pending)


def qkv_project(prompt, tokens, w_query, w_key, w_value, attn_norm, q_norm, k_norm, cos_t, sin_t, caches):
    n_batch, n_tok, d_model = tokens.shape
    n_kv = w_key.shape[1] // HEAD_DIM
    n_group = w_query.shape[1] // w_key.shape[1]
    per = 2
    cols = per * HEAD_DIM

    def whole(shape):
        return pl.BlockSpec(shape, lambda s: (0,) * len(shape))

    in_specs = [
        pl.BlockSpec((1, n_tok, d_model), lambda s: (prompt, 0, 0)),
        pl.BlockSpec((d_model, n_group * cols), lambda s: (0, s)),
        pl.BlockSpec((d_model, cols), lambda s: (0, s)),
        pl.BlockSpec((d_model, cols), lambda s: (0, s)),
        whole((1, d_model)), whole((1, HEAD_DIM)), whole((1, HEAD_DIM)),
        whole((n_tok, HEAD_DIM)), whole((n_tok, HEAD_DIM)),
    ]
    args = [tokens, w_query, w_key, w_value, attn_norm, q_norm, k_norm, cos_t, sin_t]
    aliases = {}
    if caches is not None:
        aliases = {len(args): 1, len(args) + 1: 2}
        args += list(caches)
        in_specs += [pl.BlockSpec(memory_space=pl.ANY)] * 2
    flops = 2 * n_tok * d_model * (w_query.shape[1] + 2 * w_key.shape[1])
    return pl.pallas_call(
        qkv_kernel,
        grid=(n_kv // per,),
        in_specs=in_specs,
        out_specs=[
            pl.BlockSpec((per, n_group + 2, n_tok, HEAD_DIM), lambda s: (s, 0, 0, 0)),
            pl.BlockSpec((1, n_tok, cols), lambda s: (prompt, 0, s)),
            pl.BlockSpec((1, n_tok, cols), lambda s: (prompt, 0, s)),
        ],
        out_shape=[
            jax.ShapeDtypeStruct((n_kv, n_group + 2, n_tok, HEAD_DIM), jnp.bfloat16),
            jax.ShapeDtypeStruct((n_batch, n_tok, n_kv * HEAD_DIM), jnp.bfloat16),
            jax.ShapeDtypeStruct((n_batch, n_tok, n_kv * HEAD_DIM), jnp.bfloat16),
        ],
        scratch_shapes=[pltpu.VMEM((n_tok, d_model), jnp.bfloat16)],
        input_output_aliases=aliases,
        compiler_params=pltpu.CompilerParams(vmem_limit_bytes=VMEM_LIMIT),
        cost_estimate=pl.CostEstimate(flops=flops, bytes_accessed=48 << 20, transcendentals=0),
        name="qkv",
    )(*args)


def attention_kernel(gathered, n_full_ref, q_ref, kv_ref, o_ref, qt_ref, vt_ref, m_ref, l_ref, acc_ref):
    n_group, n_tok = q_ref.shape[1], q_ref.shape[2]
    n_full = n_full_ref[0] if gathered else pl.program_id(0)
    scale = HEAD_DIM ** -0.5 * math.log2(math.e)
    lanes = 8

    def keys_of(idx):
        return kv_ref[idx, 0, 0] if gathered else kv_ref[idx, 0]

    def turn_values(idx):
        vt_ref[idx] = (kv_ref[idx, 0, 1] if gathered else kv_ref[idx, 1]).T

    if gathered:
        def turn(j, carry):
            turn_values(j)
            return carry

        lax.fori_loop(0, n_full + 1, turn, 0)
    else:
        turn_values(n_full)
    for g in range(n_group):
        qt_ref[g] = q_ref[0, g].T

    def scores_t(keys, g):
        return jnp.dot(keys, qt_ref[g], preferred_element_type=jnp.float32)

    def weighted_t(idx, probs):
        return jnp.dot(vt_ref[idx], probs.astype(jnp.bfloat16), preferred_element_type=jnp.float32)

    def partial_sum(p):
        return jnp.sum(p.reshape(n_tok // lanes, lanes, n_tok), axis=0)

    def diagonal():
        keys = keys_of(n_full)
        visible = lax.broadcasted_iota(jnp.int32, (n_tok, n_tok), 0) <= lax.broadcasted_iota(jnp.int32, (n_tok, n_tok), 1)
        for g in range(n_group):
            s = jnp.where(visible, scores_t(keys, g) * scale, -jnp.inf)
            top = jnp.max(s, axis=0, keepdims=True)
            p = jnp.exp2(s - top)
            m_ref[g] = top
            l_ref[g] = partial_sum(p)
            acc_ref[g] = weighted_t(n_full, p)

    def fixed_shift(j, carry):
        keys = keys_of(j)
        s = scores_t(keys, 0)
        for g in range(n_group):
            after = scores_t(keys, g + 1) if g + 1 < n_group else None
            p = jnp.exp2(s * scale - m_ref[g])
            l_ref[g] += partial_sum(p)
            acc_ref[g] += weighted_t(j, p)
            s = after
        return carry

    def running_max(j, carry):
        keys = keys_of(j)
        for g in range(n_group):
            s = scores_t(keys, g) * scale
            old = m_ref[g]
            top = jnp.maximum(old, jnp.max(s, axis=0, keepdims=True))
            alpha = jnp.exp2(old - top)
            p = jnp.exp2(s - top)
            m_ref[g] = top
            l_ref[g] = l_ref[g] * alpha + partial_sum(p)
            acc_ref[g] = acc_ref[g] * alpha + weighted_t(j, p)
        return carry

    diagonal()
    lax.fori_loop(0, n_full, fixed_shift, 0)

    largest = jnp.max(jnp.abs(acc_ref[...]).reshape(-1, lanes, n_tok), axis=0)
    sums = jnp.max(l_ref[...], axis=0)
    fine = jnp.where((largest < 1e36) & (sums < 1e30), 0.0, 1.0)

    @pl.when(jnp.max(fine) > 0.5)
    def _():
        diagonal()
        lax.fori_loop(0, n_full, running_max, 0)

    for g in range(n_group):
        out = acc_ref[g] / jnp.sum(l_ref[g], axis=0, keepdims=True)
        o_ref[0, :, g * HEAD_DIM:(g + 1) * HEAD_DIM] = out.T.astype(jnp.bfloat16)


def attention(qkv, kv, n_full, gathered):
    n_task, n_slot, n_tok, _ = qkv.shape
    n_group = n_slot - 2
    if gathered:
        n_piece = kv.shape[0]
        kv_spec = pl.BlockSpec((n_piece, 1, 2, n_tok, HEAD_DIM), lambda t, n: (0, t, 0, 0, 0))
    else:
        kv, n_piece = qkv, n_task
        kv_spec = pl.BlockSpec((n_piece, 2, n_tok, HEAD_DIM), lambda t, n: (0, n_group // 2, 0, 0))
    pairs = n_task * n_piece if gathered else n_task * (n_task + 1) // 2
    return pl.pallas_call(
        functools.partial(attention_kernel, gathered),
        grid_spec=pltpu.PrefetchScalarGridSpec(
            num_scalar_prefetch=1,
            grid=(n_task,),
            in_specs=[pl.BlockSpec((1, n_group, n_tok, HEAD_DIM), lambda t, n: (t, 0, 0, 0)), kv_spec],
            out_specs=pl.BlockSpec((1, n_tok, n_group * HEAD_DIM), lambda t, n: (t, 0, 0)),
            scratch_shapes=[
                pltpu.VMEM((n_group, HEAD_DIM, n_tok), jnp.bfloat16),
                pltpu.VMEM((n_piece, HEAD_DIM, n_tok), jnp.bfloat16),
                pltpu.VMEM((n_group, 1, n_tok), jnp.float32),
                pltpu.VMEM((n_group, 8, n_tok), jnp.float32),
                pltpu.VMEM((n_group, HEAD_DIM, n_tok), jnp.float32),
            ],
        ),
        out_shape=jax.ShapeDtypeStruct((n_task, n_tok, n_group * HEAD_DIM), jnp.bfloat16),
        compiler_params=pltpu.CompilerParams(vmem_limit_bytes=VMEM_LIMIT),
        cost_estimate=pl.CostEstimate(flops=2 * 4 * pairs * n_group * n_tok * n_tok * HEAD_DIM, bytes_accessed=16 << 20, transcendentals=0),
        name="attend",
    )(n_full, qkv, kv)


def out_kernel(x_ref, o_ref, w_ref, *refs):
    out_ref, flat_ref = refs[-2:]
    n_kv, _, cols = o_ref.shape

    @pl.when(pl.program_id(0) == 0)
    def _():
        for h in range(n_kv):
            flat_ref[:, h * cols:(h + 1) * cols] = o_ref[h]

    proj = jnp.dot(flat_ref[...], w_ref[...], preferred_element_type=jnp.float32)
    out_ref[0] = (x_ref[0].astype(jnp.float32) + proj).astype(jnp.bfloat16)


def out_project(prompt, tokens, heads, w_out, prev):
    n_batch, n_tok, d_model = tokens.shape
    n_kv, _, cols = heads.shape
    blk = 512
    in_specs = [
        pl.BlockSpec((1, n_tok, blk), lambda s: (prompt, 0, s)),
        pl.BlockSpec((n_kv, n_tok, cols), lambda s: (0, 0, 0)),
        pl.BlockSpec((n_kv * cols, blk), lambda s: (0, s)),
    ]
    args = [tokens, heads, w_out]
    aliases = {}
    if prev is not None:
        aliases = {3: 0}
        args.append(prev)
        in_specs.append(pl.BlockSpec(memory_space=pl.ANY))
    return pl.pallas_call(
        out_kernel,
        grid=(d_model // blk,),
        in_specs=in_specs,
        out_specs=pl.BlockSpec((1, n_tok, blk), lambda s: (prompt, 0, s)),
        out_shape=jax.ShapeDtypeStruct((n_batch, n_tok, d_model), jnp.bfloat16),
        scratch_shapes=[pltpu.VMEM((n_tok, n_kv * cols), jnp.bfloat16)],
        input_output_aliases=aliases,
        compiler_params=pltpu.CompilerParams(vmem_limit_bytes=VMEM_LIMIT),
        cost_estimate=pl.CostEstimate(flops=2 * n_tok * n_kv * cols * d_model, bytes_accessed=32 << 20, transcendentals=0),
        name="outproj",
    )(*args)


def solution(mesh):
    def per_device(tokens, w_query, w_key, w_value, w_out, attn_norm, q_norm, k_norm):
        n_batch, seq_loc, _ = tokens.shape
        n_kv = w_key.shape[1] // HEAD_DIM
        me = lax.axis_index('sp')
        cos_t, sin_t = rope_tables(me * seq_loc + jnp.arange(seq_loc))
        norms = (attn_norm.reshape(1, -1), q_norm.reshape(1, -1), k_norm.reshape(1, -1))
        n_full = me.astype(jnp.int32).reshape(1)
        caches, out, last = None, None, None
        sent, mixed = {}, {}

        def after_last(value):
            return value if last is None else lax.optimization_barrier((value, last))[0]

        def exchange(value):
            return lax.all_to_all(value, 'sp', 0, 0, tiled=True)

        for kind, b in ORDER:
            split = b < N_SPLIT
            if kind == 'qkv':
                send, kc, vc = qkv_project(b, after_last(tokens), w_query, w_key, w_value, *norms, cos_t, sin_t, caches)
                caches = (kc, vc)
                if split:
                    sent[b] = (exchange(send), None)
                else:
                    sent[b] = (send, lax.all_gather(send[:, -2:], 'sp'))
                last = send
            elif kind == 'att':
                o = attention(after_last(sent[b][0]), sent[b][1], n_full, not split)
                mixed[b] = exchange(o) if split else o
                last = o
            else:
                out = out_project(b, tokens, after_last(mixed[b]), w_out, out)
                last = out
        cache_shape = (n_batch, seq_loc, n_kv, HEAD_DIM)
        return out, caches[0].reshape(cache_shape), caches[1].reshape(cache_shape)

    spec_tok = P('dp', 'sp', None)
    spec_cache = P('dp', 'sp', None, None)
    spec_mat = P(None, None)
    spec_vec = P(None)

    return jax.shard_map(per_device, mesh=mesh, in_specs=(spec_tok, spec_mat, spec_mat, spec_mat, spec_mat, spec_vec, spec_vec, spec_vec), out_specs=(spec_tok, spec_cache, spec_cache), check_vma=False)
```

time: 2360 us -> 1210 us (0.51)
  the two profiles are of different devices: /device:TPU:81 before, /device:TPU:127 now
where the time goes in v1:
time: 1210 us
  Pallas kernels  698 us (58%)
  blocking collectives  384 us (32%)
  waiting for transfers between devices  63.8 us (5%)
  local copies, waits for them, and re-layouts  22.4 us (2%)
  starting transfers between devices  21.5 us (2%)
  between operations  14.3 us (1%)
    pallas_call x6, Pallas kernels, attention(): pl.pallas_call(functools.partial(attention_kernel, gathered), grid_spec=p...  428 us
    all_to_all x3, blocking collectives, exchange(): return lax.all_to_all(value, 'sp', 0, 0, tiled=True)  384 us
    pallas_call x6, Pallas kernels, qkv_project(): pl.pallas_call(qkv_kernel, grid=(n_kv // per,), in_specs=in_specs, out_sp...  168 us
    pallas_call x6, Pallas kernels, out_project(): pl.pallas_call(out_kernel, grid=(d_model // blk,), in_specs=in_specs, out...  102 us
    all_to_all x3, waiting for transfers between devices, exchange(): return lax.all_to_all(value, 'sp', 0, 0, tiled=True)  63.7 us
  transfers between devices with their start and end apart: 6, of which 2 were waited for; matrix products, arithmetic and copies ran while one was open for 1% of the time, Pallas kernels for 40%

profile of v1, /device:TPU:127, one launch (start us, length us, event | category | flops | bytes accessed | tf_op | source)
XLA Modules:
  0.0 1206.5 jit_solution(15116287523917789702)
XLA Ops:
  7.2 1.3 reshape.36.an_ref
  8.5 1.0 fusion
  9.5 1.0 pad_maximum_fusion
  10.5 28.0 %qkv.6 = (bf16[8,6,512,128]{3,2,1,0:T(8,128)(2,1)}, bf16[6,512,1024]{2,1,0:T(8,128)(2,1)}, bf16[6,512,1024]{2,1,0:T(8,128)(2,1)}) custom-call(bf16[6,512,2560]{2,1,0:T(8,128)(2,1)} %x_ref.18, bf16[2560,4096]{1,0:T(8,128)(2,1)} %wq_ref.11, bf16[2560,1024]{1,0:T(8,128)(2,1)} %wk_ref.11, bf16[2560,1024]{1,0:T(8,128)(2,1)} %wv_ref.11, ...), custom_call_target="tpu_custom_call" | custom-call | flops 16106127360 | bytes 50331648 | tf_op jit(solution)/shard_map/qkv/pallas_call | solution.py:113
  38.5 5.0 all-to-all-start.2
  43.5 0.2 all-gather.7.cloned.1.call-start
  43.7 28.0 %qkv.7 = (bf16[8,6,512,128]{3,2,1,0:T(8,128)(2,1)}, bf16[6,512,1024]{2,1,0:T(8,128)(2,1)}, bf16[6,512,1024]{2,1,0:T(8,128)(2,1)}) custom-call(bf16[6,512,2560]{2,1,0:T(8,128)(2,1)} %x_ref.18, bf16[2560,4096]{1,0:T(8,128)(2,1)} %wq_ref.11, bf16[2560,1024]{1,0:T(8,128)(2,1)} %wk_ref.11, ...), custom_call_target="tpu_custom_call", output_to_operand_aliasing={{1}: (9, {}), {2}: (10, {})} | custom-call | flops 16106127360 | bytes 50331648 | tf_op jit(solution)/shard_map/qkv/pallas_call | solution.py:113
  71.7 28.0 %qkv.8 = (bf16[8,6,512,128]{3,2,1,0:T(8,128)(2,1)}, bf16[6,512,1024]{2,1,0:T(8,128)(2,1)}, bf16[6,512,1024]{2,1,0:T(8,128)(2,1)}) custom-call(bf16[6,512,2560]{2,1,0:T(8,128)(2,1)} %x_ref.18, bf16[2560,4096]{1,0:T(8,128)(2,1)} %wq_ref.11, bf16[2560,1024]{1,0:T(8,128)(2,1)} %wk_ref.11, ...), custom_call_target="tpu_custom_call", output_to_operand_aliasing={{1}: (9, {}), {2}: (10, {})} | custom-call | flops 16106127360 | bytes 50331648 | tf_op jit(solution)/shard_map/qkv/pallas_call | solution.py:113
  99.7 13.3 %all-to-all-done.2.q_ref.kv_ref = bf16[8,6,512,128]{3,2,1,0:T(8,128)(2,1)} async-done(((bf16[8,6,512,128]{3,2,1,0:T(8,128)(2,1)}), bf16[8,6,512,128]{3,2,1,0:T(8,128)(2,1)}, u32[]{:S(2)}, u32[]{:S(2)}) %all-to-all-start.2) | async-done | bytes 6291488 | tf_op jit(solution)/shard_map/all_to_all | solution.py:308
  113.0 52.6 %attend.6 = bf16[8,512,512]{2,1,0:T(8,128)(2,1)} custom-call(s32[1]{0:T(128)} %bitcast.n_full_ref, bf16[8,6,512,128]{3,2,1,0:T(8,128)(2,1)} %all-to-all-done.2.q_ref.kv_ref, bf16[8,6,512,128]{3,2,1,0:T(8,128)(2,1)} %all-to-all-done.2.q_ref.kv_ref), custom_call_target="tpu_custom_call" | custom-call | flops 38654705664 | bytes 16777216 | tf_op jit(solution)/shard_map/attend/pallas_call | solution.py:229
  165.7 28.0 %qkv.9 = (bf16[8,6,512,128]{3,2,1,0:T(8,128)(2,1)}, bf16[6,512,1024]{2,1,0:T(8,128)(2,1)}, bf16[6,512,1024]{2,1,0:T(8,128)(2,1)}) custom-call(bf16[6,512,2560]{2,1,0:T(8,128)(2,1)} %x_ref.18, bf16[2560,4096]{1,0:T(8,128)(2,1)} %wq_ref.11, bf16[2560,1024]{1,0:T(8,128)(2,1)} %wk_ref.11, ...), custom_call_target="tpu_custom_call", output_to_operand_aliasing={{1}: (9, {}), {2}: (10, {})} | custom-call | flops 16106127360 | bytes 50331648 | tf_op jit(solution)/shard_map/qkv/pallas_call | solution.py:113
  193.7 3.1 slice.9
  196.8 0.1 all-gather.7.cloned.1.call-update
  196.8 0.1 all-gather.9.cloned.1.call-start
  196.9 141.6 %all_to_all.30.q_ref.kv_ref = bf16[8,6,512,128]{3,2,1,0:T(8,128)(2,1)} all-to-all(bf16[8,6,512,128]{3,2,1,0:T(8,128)(2,1)} %get-tuple-element.40), channel_id=1, replica_groups=mesh['dp'=4,'sp'=8] {'sp'}, dimensions={0} | all-to-all | bytes 12582912 | tf_op jit(solution)/shard_map/all_to_all | solution.py:308
  338.5 52.2 %attend.7 = bf16[8,512,512]{2,1,0:T(8,128)(2,1)} custom-call(s32[1]{0:T(128)} %bitcast.n_full_ref, bf16[8,6,512,128]{3,2,1,0:T(8,128)(2,1)} %all_to_all.30.q_ref.kv_ref, bf16[8,6,512,128]{3,2,1,0:T(8,128)(2,1)} %all_to_all.30.q_ref.kv_ref), custom_call_target="tpu_custom_call" | custom-call | flops 38654705664 | bytes 16777216 | tf_op jit(solution)/shard_map/attend/pallas_call | solution.py:229
  390.7 28.0 %qkv.10 = (bf16[8,6,512,128]{3,2,1,0:T(8,128)(2,1)}, bf16[6,512,1024]{2,1,0:T(8,128)(2,1)}, bf16[6,512,1024]{2,1,0:T(8,128)(2,1)}) custom-call(bf16[6,512,2560]{2,1,0:T(8,128)(2,1)} %x_ref.18, bf16[2560,4096]{1,0:T(8,128)(2,1)} %wq_ref.11, bf16[2560,1024]{1,0:T(8,128)(2,1)} %wk_ref.11, ...), custom_call_target="tpu_custom_call", output_to_operand_aliasing={{1}: (9, {}), {2}: (10, {})} | custom-call | flops 16106127360 | bytes 50331648 | tf_op jit(solution)/shard_map/qkv/pallas_call | solution.py:113
  418.7 3.2 slice.10
  421.9 0.1 all-gather.9.cloned.1.call-update
  421.9 0.1 all-gather.11.cloned.1.call-start
  422.0 144.8 %all_to_all.31.q_ref.kv_ref = bf16[8,6,512,128]{3,2,1,0:T(8,128)(2,1)} all-to-all(bf16[8,6,512,128]{3,2,1,0:T(8,128)(2,1)} %get-tuple-element.44), channel_id=1, replica_groups=mesh['dp'=4,'sp'=8] {'sp'}, dimensions={0} | all-to-all | bytes 12582912 | tf_op jit(solution)/shard_map/all_to_all | solution.py:308
  566.8 52.2 %attend.8 = bf16[8,512,512]{2,1,0:T(8,128)(2,1)} custom-call(s32[1]{0:T(128)} %bitcast.n_full_ref, bf16[8,6,512,128]{3,2,1,0:T(8,128)(2,1)} %all_to_all.31.q_ref.kv_ref, bf16[8,6,512,128]{3,2,1,0:T(8,128)(2,1)} %all_to_all.31.q_ref.kv_ref), custom_call_target="tpu_custom_call" | custom-call | flops 38654705664 | bytes 16777216 | tf_op jit(solution)/shard_map/attend/pallas_call | solution.py:229
  619.1 28.0 %qkv.11 = (bf16[8,6,512,128]{3,2,1,0:T(8,128)(2,1)}, bf16[6,512,1024]{2,1,0:T(8,128)(2,1)}, bf16[6,512,1024]{2,1,0:T(8,128)(2,1)}) custom-call(bf16[6,512,2560]{2,1,0:T(8,128)(2,1)} %x_ref.18, bf16[2560,4096]{1,0:T(8,128)(2,1)} %wq_ref.11, bf16[2560,1024]{1,0:T(8,128)(2,1)} %wk_ref.11, ...), custom_call_target="tpu_custom_call", output_to_operand_aliasing={{1}: (9, {}), {2}: (10, {})} | custom-call | flops 16106127360 | bytes 50331648 | tf_op jit(solution)/shard_map/qkv/pallas_call | solution.py:113
  647.1 3.1 slice.11
  650.2 0.1 all-gather.11.cloned.1.call-update
  650.2 98.0 %all_to_all.32.o_ref = bf16[8,512,512]{2,1,0:T(8,128)(2,1)} all-to-all(bf16[8,512,512]{2,1,0:T(8,128)(2,1)} %attend.6), channel_id=1, replica_groups=mesh['dp'=4,'sp'=8] {'sp'}, dimensions={0} | all-to-all | bytes 8388608 | tf_op jit(solution)/shard_map/all_to_all | solution.py:308
  748.2 0.0 slice-start
  748.2 9.3 all-to-all-start.4
  757.6 0.0 slice-start.1
  757.6 7.4 copy.27
  764.9 0.0 slice-done
  764.9 0.0 slice-done.1
  765.0 4.3 copy.26
  769.3 50.4 %all-to-all-done.4.o_ref = bf16[8,512,512]{2,1,0:T(8,128)(2,1)} async-done(((bf16[8,512,512]{2,1,0:T(8,128)(2,1)}), bf16[8,512,512]{2,1,0:T(8,128)(2,1)}, u32[]{:S(2)}, u32[]{:S(2)}) %all-to-all-start.4) | async-done | bytes 4194336 | tf_op jit(solution)/shard_map/all_to_all | solution.py:308
  819.7 6.8 all-to-all-start.3
  826.4 0.0 all-gather.7.cloned.1.call-done
  826.4 90.1 %attend.9.o_ref = bf16[8,512,512]{2,1,0:T(8,128)(2,1)} custom-call(s32[1]{0:T(128)} %bitcast.n_full_ref, bf16[8,6,512,128]{3,2,1,0:T(8,128)(2,1)} %get-tuple-element.60.q_ref, bf16[8,8,2,512,128]{4,3,2,1,0:T(8,128)(2,1)} %bitcast.33), custom_call_target="tpu_custom_call" | custom-call | flops 68719476736 | bytes 16777216 | tf_op jit(solution)/shard_map/attend/pallas_call | solution.py:229
  916.5 17.0 %outproj.6.refs_0_ = bf16[6,512,2560]{2,1,0:T(8,128)(2,1)} custom-call(bf16[6,512,2560]{2,1,0:T(8,128)(2,1)} %x_ref.18, bf16[8,512,512]{2,1,0:T(8,128)(2,1)} %all_to_all.32.o_ref, bf16[4096,2560]{1,0:T(8,128)(2,1)} %w_ref.11), custom_call_target="tpu_custom_call" | custom-call | flops 10737418240 | bytes 33554432 | tf_op jit(solution)/shard_map/outproj/pallas_call | solution.py:279
  933.6 17.1 %outproj.7.refs_0_ = bf16[6,512,2560]{2,1,0:T(8,128)(2,1)} custom-call(bf16[6,512,2560]{2,1,0:T(8,128)(2,1)} %x_ref.18, bf16[8,512,512]{2,1,0:T(8,128)(2,1)} %all-to-all-done.4.o_ref, bf16[4096,2560]{1,0:T(8,128)(2,1)} %w_ref.11, bf16[6,512,2560]{2,1,0:T(8,128)(2,1)} %outproj.6.refs_0_), custom_call_target="tpu_custom_call", output_to_operand_aliasing={{}: (3, {})} | custom-call | flops 10737418240 | bytes 33554432 | tf_op jit(solution)/shard_map/outproj/pallas_call | solution.py:279
  950.7 0.0 all-to-all-done.3.o_ref
  950.7 17.0 %outproj.8.refs_0_ = bf16[6,512,2560]{2,1,0:T(8,128)(2,1)} custom-call(bf16[6,512,2560]{2,1,0:T(8,128)(2,1)} %x_ref.18, bf16[8,512,512]{2,1,0:T(8,128)(2,1)} %all-to-all-done.3.o_ref, bf16[4096,2560]{1,0:T(8,128)(2,1)} %w_ref.11, bf16[6,512,2560]{2,1,0:T(8,128)(2,1)} %outproj.7.refs_0_), custom_call_target="tpu_custom_call", output_to_operand_aliasing={{}: (3, {})} | custom-call | flops 10737418240 | bytes 33554432 | tf_op jit(solution)/shard_map/outproj/pallas_call | solution.py:279
  967.7 17.0 %outproj.9.refs_0_ = bf16[6,512,2560]{2,1,0:T(8,128)(2,1)} custom-call(bf16[6,512,2560]{2,1,0:T(8,128)(2,1)} %x_ref.18, bf16[8,512,512]{2,1,0:T(8,128)(2,1)} %attend.9.o_ref, bf16[4096,2560]{1,0:T(8,128)(2,1)} %w_ref.11, bf16[6,512,2560]{2,1,0:T(8,128)(2,1)} %outproj.8.refs_0_), custom_call_target="tpu_custom_call", output_to_operand_aliasing={{}: (3, {})} | custom-call | flops 10737418240 | bytes 33554432 | tf_op jit(solution)/shard_map/outproj/pallas_call | solution.py:279
  984.8 0.0 all-gather.9.cloned.1.call-done
  984.8 90.3 %attend.10.o_ref = bf16[8,512,512]{2,1,0:T(8,128)(2,1)} custom-call(s32[1]{0:T(128)} %bitcast.n_full_ref, bf16[8,6,512,128]{3,2,1,0:T(8,128)(2,1)} %get-tuple-element.65.q_ref, bf16[8,8,2,512,128]{4,3,2,1,0:T(8,128)(2,1)} %bitcast.32), custom_call_target="tpu_custom_call" | custom-call | flops 68719476736 | bytes 16777216 | tf_op jit(solution)/shard_map/attend/pallas_call | solution.py:229
  1075.1 17.0 %outproj.10.refs_0_ = bf16[6,512,2560]{2,1,0:T(8,128)(2,1)} custom-call(bf16[6,512,2560]{2,1,0:T(8,128)(2,1)} %x_ref.18, bf16[8,512,512]{2,1,0:T(8,128)(2,1)} %attend.10.o_ref, bf16[4096,2560]{1,0:T(8,128)(2,1)} %w_ref.11, bf16[6,512,2560]{2,1,0:T(8,128)(2,1)} %outproj.9.refs_0_), custom_call_target="tpu_custom_call", output_to_operand_aliasing={{}: (3, {})} | custom-call | flops 10737418240 | bytes 33554432 | tf_op jit(solution)/shard_map/outproj/pallas_call | solution.py:279
  1092.1 0.0 all-gather.11.cloned.1.call-done
  1092.1 90.4 %attend.11.o_ref = bf16[8,512,512]{2,1,0:T(8,128)(2,1)} custom-call(s32[1]{0:T(128)} %bitcast.n_full_ref, bf16[8,6,512,128]{3,2,1,0:T(8,128)(2,1)} %get-tuple-element.66.q_ref, bf16[8,8,2,512,128]{4,3,2,1,0:T(8,128)(2,1)} %bitcast.34), custom_call_target="tpu_custom_call" | custom-call | flops 68719476736 | bytes 16777216 | tf_op jit(solution)/shard_map/attend/pallas_call | solution.py:229
  1182.5 17.0 %outproj.11 = bf16[6,512,2560]{2,1,0:T(8,128)(2,1)} custom-call(bf16[6,512,2560]{2,1,0:T(8,128)(2,1)} %x_ref.18, bf16[8,512,512]{2,1,0:T(8,128)(2,1)} %attend.11.o_ref, bf16[4096,2560]{1,0:T(8,128)(2,1)} %w_ref.11, bf16[6,512,2560]{2,1,0:T(8,128)(2,1)} %outproj.10.refs_0_), custom_call_target="tpu_custom_call", output_to_operand_aliasing={{}: (3, {})} | custom-call | flops 10737418240 | bytes 33554432 | tf_op jit(solution)/shard_map/outproj/pallas_call | solution.py:279
  (3 shorter events, 0.0 us)
Async XLA Ops:
  38.5 74.6 %all-to-all-start.2 = ((bf16[8,6,512,128]{3,2,1,0:T(8,128)(2,1)}), bf16[8,6,512,128]{3,2,1,0:T(8,128)(2,1)}, u32[]{:S(2)}, u32[]{:S(2)}) async-start(bf16[8,6,512,128]{3,2,1,0:T(8,128)(2,1)} %get-tuple-element.36), calls=%async_computation.2 | async-start | bytes 12582912 | tf_op jit(solution)/shard_map/all_to_all | solution.py:308
  43.5 782.9 %all-gather.7.cloned.1.call-start = ((), (), s32[]{:S(2)}) async-start(), calls=%async_computation.6 | async-start | bytes 18874368 | tf_op jit(solution)/shard_map/all_gather | solution.py:318
  196.8 787.9 %all-gather.9.cloned.1.call-start = ((), (), s32[]{:S(2)}) async-start(), calls=%async_computation.7 | async-start | bytes 18874368 | tf_op jit(solution)/shard_map/all_gather | solution.py:318
  421.9 670.2 %all-gather.11.cloned.1.call-start = ((), (), s32[]{:S(2)}) async-start(), calls=%async_computation.8 | async-start | bytes 18874368 | tf_op jit(solution)/shard_map/all_gather | solution.py:318
  748.2 16.7 %slice-start = ((s8[6291456]{0:T(1024)(128)(4,1)}), s8[2097152]{0:T(1024)(128)(4,1)S(1)}, s32[]{:S(2)}) async-start(s8[6291456]{0:T(1024)(128)(4,1)} %bitcast.14), calls=%async_computation.9 | async-start | bytes 4194304
  748.2 71.4 %all-to-all-start.4 = ((bf16[8,512,512]{2,1,0:T(8,128)(2,1)}), bf16[8,512,512]{2,1,0:T(8,128)(2,1)}, u32[]{:S(2)}, u32[]{:S(2)}) async-start(bf16[8,512,512]{2,1,0:T(8,128)(2,1)} %attend.7), calls=%async_computation.4 | async-start | bytes 8388608 | tf_op jit(solution)/shard_map/all_to_all | solution.py:308
  757.6 7.4 slice-start.1
  819.7 131.0 %all-to-all-start.3 = ((bf16[8,512,512]{2,1,0:T(8,128)(2,1)}), bf16[8,512,512]{2,1,0:T(8,128)(2,1)}, u32[]{:S(2)}, u32[]{:S(2)}) async-start(bf16[8,512,512]{2,1,0:T(8,128)(2,1)} %attend.8), calls=%async_computation.3 | async-start | bytes 8388608 | tf_op jit(solution)/shard_map/all_to_all | solution.py:308
Sparse Core Ops, SparseCore 0:
  196.9 147.0 all-gather.6
  422.0 149.4 all-gather.8
  650.3 145.1 all-gather.10
